TPU v7x, 512 devices: a 8x2x16 block of a 8x8x16 slice. The times are simulated.
512 devices in a mesh: groups: 2 (over y), seq: 128 (over z, x), tp: 2 (over core).
Axes of the slice: x: 8, y: 2, z: 16, core: 2. Of those that a mesh axis runs over, the one named last changes fastest.
The devices are a block of a 8x8x16 slice.
Arguments:
- stream: bfloat16 [2048, 6144], P(('groups', 'seq'), 'tp'), parts along dimension 0, may hold values from -6 to 6
- queries: bfloat16 [2048, 6144], P(('groups', 'seq'), 'tp'), parts along dimension 0, may hold values from -6 to 6
- key_rows: bfloat16 [2048, 1024], P(('groups', 'seq'), 'tp'), parts along dimension 0, may hold values from -6 to 6
- value_rows: bfloat16 [2048, 1024], P(('groups', 'seq'), 'tp'), parts along dimension 0, may hold values from -6 to 6
- routes: int32 [2048, 2], P(('groups', 'seq')), parts along dimension 0, may hold values from 0 to 3, all different within a row; in each aligned block of 8 rows (0 to 7, 8 to 15, ...) at most 4 rows name the same one
- seq_length: int32 [2], P('groups'), parts along dimension 0, may hold values from 256 to 1024
- norm_gain: float32 [6144], P('tp'), may hold values from 0.25 to 1.75
- router: float32 [6144, 4], P('tp'), may hold values from -0.078125 to 0.078125
- w_up: bfloat16 [6144, 32768], P('tp', 'seq'), may hold values from -0.078125 to 0.078125
- w_down: bfloat16 [32768, 6144], P('seq', 'tp'), may hold values from -0.0625 to 0.0625
- final_gain: float32 [6144], P('tp'), may hold values from 0.25 to 1.75
- value_weight: float32 [6144], P('tp'), may hold values from -0.078125 to 0.078125
- value_bias: float32 [1], replicated, may hold values from -3 to 3
Outputs:
- layer_out: bfloat16 [2048, 6144], P(('groups', 'seq'), 'tp'), parts along dimension 0
- values: float32 [2048], P(('groups', 'seq')), parts along dimension 0
There are 2 independent parts, one for each index of `groups`. A program takes and returns all parts, laid end to end along the dimension named above; an argument that names none is the same for every part. Nothing has to cross between parts.
Inputs may be any that keep to these rules, and one draw needn't show every extreme that they name: `routes`: each row names two different experts; among the rows on one device no expert is named more than 4 times, and some device's rows name some expert exactly 4 times.
All inputs are finite; a program needn't handle non-finite values.
Results may differ from a plain program's by a relative error of at most 0.01.
Values may be sent and summed in bfloat16 or wider, within the bound.
A program may use at most 64 MiB of HBM per device.

v0:
```python
import math
import jax
import jax.numpy as jnp
from jax import lax
from jax.sharding import Mesh
from jax.sharding import PartitionSpec as P

D = 6144
HD = 128
EXPERTS = 4
SEQ = ("seq_0", "seq_1")
GROUPS_SEQ = ("groups", "seq_0", "seq_1")
eps = 1e-05
masked = -1e30


def sent_together(arrays, axis, dim, along):
    both = jnp.concatenate(arrays, axis=along)
    result, at, done = (lax.all_gather(both, axis, axis=dim, tiled=True), 0, [])
    for a in arrays:
        done.append(lax.slice_in_dim(result, at, at + a.shape[along], axis=along))
        at += a.shape[along]
    return tuple(done)


def over_pieces(array, axis):
    pieces = lax.all_gather(array, axis)
    return pieces.sum(axis=0)


def from_everyone(array, axis):
    length = lax.axis_size(axis)
    return lax.all_to_all(
        jnp.broadcast_to(array[None], (length, *array.shape)), axis, 0, 0, tiled=True
    )


def of_everyone(array, axis):
    return from_everyone(array, axis).astype(jnp.float32).sum(axis=0)


def laid_out(pieces, dim):
    lengths = list(pieces.shape[1:])
    lengths[dim] *= pieces.shape[0]
    return jnp.moveaxis(pieces, 0, dim).reshape(lengths)


def stacked_from(array, axes, sequence):
    pieces = array
    for k in sequence:
        pieces = lax.all_gather(pieces, axes[k])
    done = sequence[::-1]
    back = [done.index(k) for k in range(len(axes))]
    pieces = pieces.transpose(*back, *range(len(axes), pieces.ndim))
    return pieces.reshape(-1, *array.shape)


def whole_of(array, axes, sequence, dim):
    return laid_out(stacked_from(array, axes, sequence), dim)


def on_device(
    stream,
    queries,
    key_rows,
    value_rows,
    routes,
    seq_length,
    norm_gain,
    router,
    w_up,
    w_down,
    final_gain,
    value_weight,
    value_bias,
):
    row_count = stream.shape[0]
    half_width = stream.shape[1]
    seq_devices = lax.axis_size(SEQ)
    owners = seq_devices // EXPERTS
    my_index = lax.axis_index(SEQ)
    seq_limit = seq_length[0]
    positions = my_index * row_count + jnp.arange(row_count, dtype=jnp.int32)
    kv_heads = key_rows.shape[1] // HD
    per_group = queries.shape[1] // HD // kv_heads
    grouped = queries.reshape(row_count, kv_heads, per_group, HD)
    inv_root = 1.0 / math.sqrt(HD)
    slot_cap = row_count // 2
    run_max = jnp.full((kv_heads, per_group, row_count), masked, jnp.float32)
    key_block, value_block = sent_together((key_rows, value_rows), SEQ, 0, 1)
    key_count = key_block.shape[0]
    scores = (
        jnp.einsum(
            "qkgd,ckd->kgqc",
            grouped,
            key_block.reshape(key_count, kv_heads, HD),
            preferred_element_type=jnp.float32,
        )
        * inv_root
    )
    key_pos = jnp.arange(key_count, dtype=jnp.int32)
    allowed = (key_pos[None, :] <= positions[:, None]) & (key_pos[None, :] < seq_limit)
    scores = jnp.where(allowed, scores, masked)
    new_max = jnp.maximum(run_max, jnp.max(scores, axis=-1))
    weights = jnp.where(allowed, jnp.exp(scores - new_max[..., None]), 0.0)
    new_sum = jnp.sum(weights, axis=-1)
    update = jnp.einsum(
        "kgqc,ckd->kgqd",
        weights.astype(jnp.bfloat16),
        value_block.reshape(key_count, kv_heads, HD),
        preferred_element_type=jnp.float32,
    )
    attended = (update / new_sum[..., None]).transpose(2, 0, 1, 3).reshape(row_count, half_width)
    hidden = stream.astype(jnp.float32) + attended
    gained = hidden * norm_gain
    squares = jnp.sum(hidden * hidden, axis=1)
    total_sq, raw_logits = (over_pieces(squares, "tp"), over_pieces(jnp.dot(gained, router), "tp"))
    norm_scale = lax.rsqrt(total_sq / D + eps)
    normed = gained * norm_scale[:, None]
    logits = raw_logits * norm_scale[:, None]
    normed_half = normed.astype(jnp.bfloat16)
    expert_ids = jnp.arange(EXPERTS, dtype=jnp.int32)
    chosen = (routes[:, :, None] == expert_ids).astype(jnp.float32)
    picked = jnp.sum(chosen * logits[:, None, :], axis=2)
    gates = jax.nn.sigmoid(picked - picked[:, ::-1])
    flat_hits = chosen.reshape(row_count * 2, EXPERTS)
    earlier = jnp.cumsum(flat_hits, axis=0) - flat_hits
    slot_index = jnp.sum(earlier * flat_hits, axis=1).astype(jnp.int32)
    target = routes.reshape(row_count * 2) * slot_cap + slot_index
    placing = (target[:, None] == jnp.arange(EXPERTS * slot_cap, dtype=jnp.int32)[None, :]).astype(
        jnp.bfloat16
    )
    every_row = lax.all_gather(normed_half, SEQ, axis=0, tiled=True)
    every_route = whole_of(routes, SEQ, (0, 1), 0)
    my_expert = my_index // owners
    row_hits = jnp.sum((every_route == my_expert).astype(jnp.int32), axis=1).reshape(
        seq_devices, row_count
    )
    ranks = jnp.cumsum(row_hits, axis=1) - row_hits
    selector = (
        (ranks[:, :, None] == jnp.arange(slot_cap, dtype=jnp.int32)[None, None, :])
        & (row_hits[:, :, None] > 0)
    ).astype(jnp.bfloat16)
    arrived = jnp.einsum(
        "src,srd->scd",
        selector,
        every_row.reshape(seq_devices, row_count, half_width),
        preferred_element_type=jnp.float32,
    ).astype(jnp.bfloat16)
    lead = arrived.shape[0]
    items = arrived.shape[1]
    flat_rows = arrived.reshape(lead * items, half_width)
    up_part = jnp.dot(flat_rows, w_up, preferred_element_type=jnp.float32)
    up_total = of_everyone(up_part.astype(jnp.bfloat16), "tp").astype(jnp.float32)
    active = jax.nn.silu(up_total).astype(jnp.bfloat16)
    down_part = jnp.dot(active, w_down, preferred_element_type=jnp.float32).astype(jnp.bfloat16)
    partial_out = down_part.reshape(lead, items, half_width)
    returned = lax.all_to_all(partial_out, SEQ, split_axis=0, concat_axis=0, tiled=True)
    summed = jnp.sum(
        returned.reshape(EXPERTS, owners, slot_cap, half_width), axis=1, dtype=jnp.float32
    ).reshape(EXPERTS * slot_cap, half_width)
    fetched = jnp.dot(placing.astype(jnp.float32), summed)
    mixed = jnp.sum(fetched.reshape(row_count, 2, half_width) * gates[:, :, None], axis=1)
    final = hidden + mixed
    sq_part = jnp.sum(final * final, axis=1)
    dot_part = jnp.sum(final * (final_gain * value_weight), axis=1)
    sq_total, dot_total = (over_pieces(sq_part, "tp"), over_pieces(dot_part, "tp"))
    estimate = dot_total * lax.rsqrt(sq_total / D + eps) + value_bias[0]
    estimate = jnp.where(positions < seq_limit, estimate, 0.0)
    return (final.astype(jnp.bfloat16), estimate)


def solution(mesh):
    finer = Mesh(
        mesh.devices.reshape(mesh.shape["groups"], 16, 8, mesh.shape["tp"]),
        ("groups", "seq_0", "seq_1", "tp"),
    )
    placed = (
        P(GROUPS_SEQ, "tp"),
        P(GROUPS_SEQ, "tp"),
        P(GROUPS_SEQ, "tp"),
        P(GROUPS_SEQ, "tp"),
        P(GROUPS_SEQ, None),
        P("groups"),
        P("tp"),
        P("tp", None),
        P("tp", SEQ),
        P(SEQ, "tp"),
        P("tp"),
        P("tp"),
        P(),
    )
    return jax.shard_map(
        on_device,
        mesh=finer,
        in_specs=placed,
        out_specs=(P(GROUPS_SEQ, "tp"), P(GROUPS_SEQ)),
        check_vma=False,
    )
```

profile of v0, /device:TPU:65, one launch (start us, length us, event | category | flops | bytes accessed | tf_op | source)
XLA Modules:
  0.0 552.6 jit_solution(5043075534300548686)
XLA Ops:
  7.2 0.0 copy-start
  7.2 0.1 all-gather.11.cloned.1.call-start
  7.3 1.4 pad_maximum_fusion
  8.7 0.1 all-gather.11.cloned.1.call-update
  8.7 0.1 all-gather.13.cloned.1.call-start
  9.5 1.3 dynamic-slice
  11.4 0.1 fusion.23
  11.5 169.5 %all-gather.11.cloned.1.call-done = bf16[1024,1024]{1,0:T(8,128)(2,1)} async-done(((bf16[8,1024]{1,0:T(8,128)(2,1)}), bf16[1024,1024]{1,0:T(8,128)(2,1)}) %all-gather.11.cloned.1.call-update) | async-done | bytes 2097168 | tf_op jit(solution)/shard_map/all_gather | solution.py:19
  181.0 2.7 fusion.32
  183.7 2.3 copy.70
  186.0 0.0 copy-done.7
  186.0 1.6 fusion.33
  187.5 0.0 copy-start.1
  187.6 0.0 copy-start.2
  187.6 0.0 copy-start.6
  187.6 1.3 copy.71
  188.9 0.3 fusion.9
  189.2 1.7 fusion.8
  190.9 0.0 copy-done.1
  190.9 0.1 multiply_reduce_fusion.2
  191.1 0.2 dynamic-update-slice
  191.3 12.9 %all-reduce = f32[16]{0:T(128)S(1)} all-reduce(f32[16]{0:T(128)S(1)} %dynamic-update-slice), channel_id=4, replica_groups=mesh['groups'=2,'seq_0'=16,'seq_1'=8,'tp'=2] {'tp'}, use_global_device_ids=true, to_apply=%add | all-reduce | flops 16 | bytes 128
  204.2 0.1 reshape.141
  204.3 0.0 copy-done.2
  204.3 0.7 multiply_convert_fusion.2
  205.0 0.1 all-gather.13.cloned.1.call-update
  205.1 0.0 copy-done.6
  205.1 20.9 %all-gather.6 = s32[16,8,2]{1,2,0:T(2,128)S(1)} all-gather(s32[1,8,2]{1,2,0:T(2,128)S(1)} %bitcast.63), channel_id=2, replica_groups=mesh['groups'=2,'seq_0'=16,'seq_1'=8,'tp'=2] {'seq_0'}, dimensions={0}, use_global_device_ids=true | all-gather | bytes 1088 | tf_op jit(solution)/shard_map/all_gather | solution.py:51
  226.0 19.8 %all-gather.1 = s32[128,8,2]{1,2,0:T(2,128)S(1)} all-gather(s32[16,8,2]{1,2,0:T(2,128)S(1)} %all-gather.6), channel_id=3, replica_groups=mesh['groups'=2,'seq_0'=16,'seq_1'=8,'tp'=2] {'seq_1'}, dimensions={0}, use_global_device_ids=true | all-gather | bytes 9216 | tf_op jit(solution)/shard_map/all_gather | solution.py:51
  245.7 0.2 fusion.18
  245.9 0.1 copy.59
  246.0 0.1 reduce_window_sum.25
  246.2 0.1 copy.60
  246.3 0.1 copy.61
  246.4 96.1 %all-gather.13.cloned.1.call-done = bf16[1024,3072]{1,0:T(8,128)(2,1)} async-done(((bf16[8,3072]{1,0:T(8,128)(2,1)}), bf16[1024,3072]{1,0:T(8,128)(2,1)}) %all-gather.13.cloned.1.call-update) | async-done | bytes 6291472 | tf_op jit(solution)/shard_map/all_gather | solution.py:133
  342.5 6.3 %fusion.2 = bf16[128,4,3072]{2,1,0:T(4,128)(2,1)} fusion(bf16[1024,3072]{1,0:T(8,128)(2,1)} %all-gather.13.cloned.1.call-done, s32[128,8]{1,0:T(8,128)S(1)} %copy.60, pred[128,8]{1,0:T(8,128)(4,1)S(1)} %copy.61), kind=kOutput, calls=%fused_computation.3 | convolution fusion | flops 26746880 | bytes 9442304 | tf_op jit(solution)/shard_map/src,srd->scd/dot_general | solution.py:144
  348.8 5.9 %reshape.135 = bf16[512,3072]{1,0:T(8,128)(2,1)} reshape(bf16[128,4,3072]{2,1,0:T(4,128)(2,1)} %fusion.2) | data formatting | bytes 6291456 | tf_op jit(solution)/shard_map/reshape | solution.py:152
  354.7 3.3 convolution_convert_fusion.1
  358.1 11.9 %all_to_all.10 = bf16[2,512,256]{2,1,0:T(8,128)(2,1)S(1)} all-to-all(bf16[2,512,256]{2,1,0:T(8,128)(2,1)S(1)} %broadcast_in_dim.23), channel_id=1, replica_groups=mesh['groups'=2,'seq_0'=16,'seq_1'=8,'tp'=2] {'tp'}, dimensions={0} | all-to-all | bytes 1048576 | tf_op jit(solution)/shard_map/all_to_all | solution.py:33
  370.0 0.1 convert_reduce_fusion.1
  370.1 0.0 copy-done
  370.1 2.7 convolution_convert_fusion
  372.8 6.1 %reshape.136 = bf16[128,4,3072]{2,1,0:T(4,128)(2,1)} reshape(bf16[512,3072]{1,0:T(8,128)(2,1)} %convolution_convert_fusion) | data formatting | bytes 6291456 | tf_op jit(solution)/shard_map/reshape | solution.py:157
  378.9 17.0 %all-to-all-start.1 = ((bf16[128,4,3072]{2,1,0:T(4,128)(2,1)}), bf16[128,4,3072]{2,1,0:T(4,128)(2,1)}, u32[]{:S(2)}, u32[]{:S(2)}) async-start(bf16[128,4,3072]{2,1,0:T(4,128)(2,1)} %reshape.136), calls=%async_computation.1 | async-start | bytes 6291456 | tf_op jit(solution)/shard_map/all_to_all | solution.py:158
  395.9 0.1 copy.55
  396.0 0.1 eq.72
  396.1 0.1 fusion.24
  396.2 0.2 select_reduce_fusion
  396.4 0.1 convert_element_type.59
  396.5 0.1 copy.57
  397.2 0.0 copy-done.4
  397.2 0.0 copy-done.5
  397.2 0.1 convolution_bitcast_fusion.1
  397.4 2.2 all-gather.7
  399.6 132.8 %all-to-all-done.1 = bf16[128,4,3072]{2,1,0:T(4,128)(2,1)} async-done(((bf16[128,4,3072]{2,1,0:T(4,128)(2,1)}), bf16[128,4,3072]{2,1,0:T(4,128)(2,1)}, u32[]{:S(2)}, u32[]{:S(2)}) %all-to-all-start.1) | async-done | bytes 3145760 | tf_op jit(solution)/shard_map/all_to_all | solution.py:158
  532.5 3.2 convert_reduce_fusion
  535.7 0.2 fusion.7
  535.9 0.8 multiply_reduce_fusion
  536.7 0.2 dynamic-update-slice.2
  536.9 0.2 dynamic-update-slice.1
  537.1 7.9 %all-reduce.3 = (f32[16]{0:T(128)S(1)}, f32[16]{0:T(128)S(1)}) all-reduce(f32[16]{0:T(128)S(1)} %dynamic-update-slice.1, f32[16]{0:T(128)S(1)} %dynamic-update-slice.2), channel_id=6, replica_groups=mesh['groups'=2,'seq_0'=16,'seq_1'=8,'tp'=2] {'tp'}, use_global_device_ids=true, to_apply=%add.1 | all-reduce | flops 32 | bytes 256
  545.0 0.1 reshape.143
  545.1 0.1 reshape.144
  545.2 0.5 compare_select_fusion
  (29 shorter events, 0.3 us)
Async XLA Ops:
  7.2 362.9 %copy-start = (bf16[256,3072]{1,0:T(8,128)(2,1)S(1)}, bf16[256,3072]{1,0:T(8,128)(2,1)}, u32[]{:S(2)}) copy-start(bf16[256,3072]{1,0:T(8,128)(2,1)} %param.22) | copy-start | bytes 4718596
  7.2 173.8 %all-gather.11.cloned.1.call-start = ((), (), s32[]{:S(2)}) async-start(), calls=%async_computation.2 | async-start | bytes 2113536 | tf_op jit(solution)/shard_map/all_gather | solution.py:19
  8.7 333.8 %all-gather.13.cloned.1.call-start = ((), (), s32[]{:S(2)}) async-start(), calls=%async_computation.3 | async-start | bytes 6340608 | tf_op jit(solution)/shard_map/all_gather | solution.py:133
  11.5 174.5 %copy-start.7 = (bf16[8,3072]{1,0:T(8,128)(2,1)S(1)}, bf16[8,3072]{1,0:T(8,128)(2,1)}, u32[]{:S(2)}) copy-start(bf16[8,3072]{1,0:T(8,128)(2,1)} %param.14) | copy-start | bytes 147460
  187.5 3.4 copy-start.1
  187.6 16.7 %copy-start.2 = (f32[3072]{0:T(1024)S(1)}, f32[3072]{0:T(1024)}, u32[]{:S(2)}) copy-start(f32[3072]{0:T(1024)} %param.19) | copy-start | bytes 36868
  187.6 17.5 %copy-start.6 = (s32[8,2]{0,1:T(2,128)S(1)}, s32[8,2]{0,1:T(2,128)}, u32[]{:S(2)}) copy-start(s32[8,2]{0,1:T(2,128)} %param.17) | copy-start | bytes 196
  378.9 18.3 %copy-start.4 = (f32[3072]{0:T(1024)S(1)}, f32[3072]{0:T(1024)}, u32[]{:S(2)}) copy-start(f32[3072]{0:T(1024)} %param.23) | copy-start | bytes 36868
  378.9 18.3 %copy-start.5 = (f32[3072]{0:T(1024)S(1)}, f32[3072]{0:T(1024)}, u32[]{:S(2)}) copy-start(f32[3072]{0:T(1024)} %param.24) | copy-start | bytes 36868
  378.9 18.3 %copy-start.3 = (f32[3072,4]{0,1:T(4,128)S(1)}, f32[3072,4]{0,1:T(4,128)}, u32[]{:S(2)}) copy-start(f32[3072,4]{0,1:T(4,128)} %param.20) | copy-start | bytes 147460
  378.9 153.6 %all-to-all-start.1 = ((bf16[128,4,3072]{2,1,0:T(4,128)(2,1)}), bf16[128,4,3072]{2,1,0:T(4,128)(2,1)}, u32[]{:S(2)}, u32[]{:S(2)}) async-start(bf16[128,4,3072]{2,1,0:T(4,128)(2,1)} %reshape.136), calls=%async_computation.1 | async-start | bytes 6291456 | tf_op jit(solution)/shard_map/all_to_all | solution.py:158
Sparse Core Ops, SparseCore 0:
  11.6 169.3 all-gather.10
  205.2 137.3 all-gather.12
where the time goes:
time: 553 us
  waiting for transfers between devices  399 us (72%)
  blocking collectives  75.5 us (14%)
  local copies, waits for them, and re-layouts  21.4 us (4%)
  starting transfers between devices  17.1 us (3%)
  between operations  16.3 us (3%)
  matrix products  15.9 us (3%)
  other arithmetic  7.87 us (1%)
    all_gather x1, waiting for transfers between devices, sent_together(): result, at, done = (lax.all_gather(both, axis, axis=dim, tiled=True), 0, [])  170 us
    all_to_all x1, waiting for transfers between devices, on_device(): lax.all_to_all(partial_out, SEQ, split_axis=0, concat_axis=0, tiled=True)  133 us
    all_gather x1, waiting for transfers between devices, on_device(): every_row = lax.all_gather(normed_half, SEQ, axis=0, tiled=True)  96.1 us
    all_gather x2, blocking collectives, stacked_from(): pieces = lax.all_gather(pieces, axes[k])  40.7 us
    unnamed x2, blocking collectives  20.7 us
    all_to_all x1, starting transfers between devices, on_device(): lax.all_to_all(partial_out, SEQ, split_axis=0, concat_axis=0, tiled=True)  17 us
    all_to_all x1, blocking collectives, from_everyone(): lax.all_to_all(jnp.broadcast_to(array[None], (length, *array.shape)), axi...  11.9 us
  transfers between devices with their start and end apart: 3, of which 3 were waited for; matrix products, arithmetic and copies ran while one was open for 1% of the time, Pallas kernels for 0%

commit v1 on v0

--- a/solution.py
+++ b/solution.py
@@ -12,6 +12,13 @@
 GROUPS_SEQ = ("groups", "seq_0", "seq_1")
 eps = 1e-05
 masked = -1e30
+
+
+def gather_over(x, axis, dim):
+    devices = lax.axis_size(axis)
+    blocks = jnp.stack([x for _ in range(devices)])
+    blocks = lax.all_to_all(blocks, axis, split_axis=0, concat_axis=0)
+    return jnp.concatenate(blocks, axis=dim)
 
 
 def sent_together(arrays, axis, dim, along):
@@ -130,7 +137,7 @@
     placing = (target[:, None] == jnp.arange(EXPERTS * slot_cap, dtype=jnp.int32)[None, :]).astype(
         jnp.bfloat16
     )
-    every_row = lax.all_gather(normed_half, SEQ, axis=0, tiled=True)
+    every_row = gather_over(normed_half, SEQ, 0)
     every_route = whole_of(routes, SEQ, (0, 1), 0)
     my_expert = my_index // owners
     row_hits = jnp.sum((every_route == my_expert).astype(jnp.int32), axis=1).reshape(

time: 553 us -> 748 us (1.35)
  blocking collectives: 75.5 us -> 344 us
  waiting for transfers between devices: 399 us -> 303 us
  starting transfers between devices: 17.1 us -> 35.4 us
    all_gather x2, blocking collectives: 40.7 us -> 306 us  [stacked_from(): pieces = lax.all_gather(pieces, axes[k])]
    all_gather x1 -> x0, waiting for transfers between devices: 96.1 us -> none  [on_device(): every_row = lax.all_gather(normed_half, SEQ, axis=0, tiled=True)]
    all_to_all x0 -> x1, starting transfers between devices: none -> 17 us  [gather_over(): blocks = lax.all_to_all(blocks, axis, split_axis=0, concat_axis=0)]
  transfers between devices with their start and end apart: 3 -> 3, of which waited for: 3 -> 2; matrix products, arithmetic and copies ran while one was open for 1% -> 0% of each run, Pallas kernels for 0% -> 0%
where the time goes in v1:
time: 748 us; the launch traced here: 747 us
  blocking collectives  344 us (46%)
  waiting for transfers between devices  303 us (41%)
  starting transfers between devices  35.4 us (5%)
  local copies, waits for them, and re-layouts  24.8 us (3%)
  between operations  16.3 us (2%)
  matrix products  15.9 us (2%)
    all_gather x2, blocking collectives, stacked_from(): pieces = lax.all_gather(pieces, axes[k])  306 us
    all_gather x1, waiting for transfers between devices, sent_together(): result, at, done = (lax.all_gather(both, axis, axis=dim, tiled=True), 0, [])  170 us
    all_to_all x1, waiting for transfers between devices, on_device(): lax.all_to_all(partial_out, SEQ, split_axis=0, concat_axis=0, tiled=True)  133 us
    unnamed x2, blocking collectives  20.8 us
    all_to_all x1, starting transfers between devices, on_device(): lax.all_to_all(partial_out, SEQ, split_axis=0, concat_axis=0, tiled=True)  18.4 us
    all_to_all x1, starting transfers between devices, gather_over(): blocks = lax.all_to_all(blocks, axis, split_axis=0, concat_axis=0)  17 us
    all_to_all x1, blocking collectives, from_everyone(): lax.all_to_all(jnp.broadcast_to(array[None], (length, *array.shape)), axi...  15.9 us
  transfers between devices with their start and end apart: 3, of which 2 were waited for; matrix products, arithmetic and copies ran while one was open for 0% of the time, Pallas kernels for 0%

profile of v1, /device:TPU:65, one launch (start us, length us, event | category | flops | bytes accessed | tf_op | source)
XLA Modules:
  0.0 746.6 jit_solution(14815669479328756627)
XLA Ops:
  7.2 0.0 copy-start
  7.2 0.1 all-gather.10.cloned.1.call-start
  7.3 1.4 pad_maximum_fusion
  8.7 0.1 all-gather.10.cloned.1.call-update
  9.4 1.3 dynamic-slice
  11.4 0.1 fusion.18
  11.4 169.6 %all-gather.10.cloned.1.call-done = bf16[1024,1024]{1,0:T(8,128)(2,1)} async-done(((bf16[8,1024]{1,0:T(8,128)(2,1)}), bf16[1024,1024]{1,0:T(8,128)(2,1)}) %all-gather.10.cloned.1.call-update) | async-done | bytes 2097168 | tf_op jit(solution)/shard_map/all_gather | solution.py:26
  181.0 2.7 fusion.27
  183.7 2.3 copy.70
  186.0 0.0 copy-done.7
  186.0 1.6 fusion.28
  187.5 0.0 copy-start.1
  187.6 0.0 copy-start.2
  187.6 1.3 copy.71
  188.9 0.3 fusion.4
  189.2 1.7 fusion.3
  190.9 0.0 copy-done.1
  190.9 0.1 multiply_reduce_fusion.2
  191.1 0.2 dynamic-update-slice
  191.3 12.9 %all-reduce = f32[16]{0:T(128)S(1)} all-reduce(f32[16]{0:T(128)S(1)} %dynamic-update-slice), channel_id=4, replica_groups=mesh['groups'=2,'seq_0'=16,'seq_1'=8,'tp'=2] {'tp'}, use_global_device_ids=true, to_apply=%add | all-reduce | flops 16 | bytes 128
  204.2 0.1 reshape.139
  204.3 0.0 copy-done.2
  204.3 0.1 multiply_convert_fusion.2
  204.4 3.4 stack.2
  207.8 17.0 %all-to-all-start = ((bf16[128,8,3072]{2,1,0:T(8,128)(2,1)}), bf16[128,8,3072]{2,1,0:T(8,128)(2,1)}, u32[]{:S(2)}, u32[]{:S(2)}) async-start(bf16[128,8,3072]{2,1,0:T(8,128)(2,1)} %stack.2), calls=%async_computation | async-start | bytes 12582912 | tf_op jit(solution)/shard_map/all_to_all | solution.py:20
  224.8 0.0 copy-done.6
  224.8 285.7 %all-gather.6 = s32[16,8,2]{1,2,0:T(2,128)S(1)} all-gather(s32[1,8,2]{1,2,0:T(2,128)S(1)} %bitcast.59), channel_id=2, replica_groups=mesh['groups'=2,'seq_0'=16,'seq_1'=8,'tp'=2] {'seq_0'}, dimensions={0}, use_global_device_ids=true | all-gather | bytes 1088 | tf_op jit(solution)/shard_map/all_gather | solution.py:58
  510.5 19.9 %all-gather.1 = s32[128,8,2]{1,2,0:T(2,128)S(1)} all-gather(s32[16,8,2]{1,2,0:T(2,128)S(1)} %all-gather.6), channel_id=3, replica_groups=mesh['groups'=2,'seq_0'=16,'seq_1'=8,'tp'=2] {'seq_1'}, dimensions={0}, use_global_device_ids=true | all-gather | bytes 9216 | tf_op jit(solution)/shard_map/all_gather | solution.py:58
  530.4 0.2 fusion.13
  530.6 0.1 copy.59
  530.7 0.1 reduce_window_sum.25
  530.8 0.1 copy.60
  531.0 0.1 copy.61
  531.1 0.0 all-to-all-done
  531.1 6.3 convolution_convert_fusion.1
  537.4 5.9 reshape.133
  543.2 3.3 convolution_convert_fusion.2
  546.6 15.9 %all_to_all.15 = bf16[2,512,256]{2,1,0:T(8,128)(2,1)S(1)} all-to-all(bf16[2,512,256]{2,1,0:T(8,128)(2,1)S(1)} %broadcast_in_dim.23), channel_id=1, replica_groups=mesh['groups'=2,'seq_0'=16,'seq_1'=8,'tp'=2] {'tp'}, dimensions={0} | all-to-all | bytes 1048576 | tf_op jit(solution)/shard_map/all_to_all | solution.py:40
  562.6 0.1 convert_reduce_fusion.1
  562.6 0.0 copy-done
  562.6 2.7 convolution_convert_fusion
  565.4 6.1 reshape.134
  571.5 18.4 %all-to-all-start.2 = ((bf16[128,4,3072]{2,1,0:T(4,128)(2,1)}), bf16[128,4,3072]{2,1,0:T(4,128)(2,1)}, u32[]{:S(2)}, u32[]{:S(2)}) async-start(bf16[128,4,3072]{2,1,0:T(4,128)(2,1)} %reshape.134), calls=%async_computation.2 | async-start | bytes 6291456 | tf_op jit(solution)/shard_map/all_to_all | solution.py:165
  589.9 0.1 copy.55
  590.0 0.1 eq.72
  590.0 0.1 fusion.19
  590.2 0.2 select_reduce_fusion
  590.4 0.1 convert_element_type.59
  590.4 0.1 copy.57
  591.2 0.0 copy-done.4
  591.2 0.0 copy-done.5
  591.2 0.0 copy-done.3
  591.2 0.1 convolution_bitcast_fusion.1
  591.4 2.1 all-gather.7
  593.5 132.9 %all-to-all-done.2 = bf16[128,4,3072]{2,1,0:T(4,128)(2,1)} async-done(((bf16[128,4,3072]{2,1,0:T(4,128)(2,1)}), bf16[128,4,3072]{2,1,0:T(4,128)(2,1)}, u32[]{:S(2)}, u32[]{:S(2)}) %all-to-all-start.2) | async-done | bytes 3145760 | tf_op jit(solution)/shard_map/all_to_all | solution.py:165
  726.4 3.2 convert_reduce_fusion
  729.7 0.2 fusion.2
  729.9 0.8 multiply_reduce_fusion
  730.7 0.2 dynamic-update-slice.2
  730.9 0.2 dynamic-update-slice.1
  731.1 7.9 %all-reduce.3 = (f32[16]{0:T(128)S(1)}, f32[16]{0:T(128)S(1)}) all-reduce(f32[16]{0:T(128)S(1)} %dynamic-update-slice.1, f32[16]{0:T(128)S(1)} %dynamic-update-slice.2), channel_id=6, replica_groups=mesh['groups'=2,'seq_0'=16,'seq_1'=8,'tp'=2] {'tp'}, use_global_device_ids=true, to_apply=%add.1 | all-reduce | flops 32 | bytes 256
  739.0 0.1 reshape.141
  739.1 0.1 reshape.142
  739.2 0.5 compare_select_fusion
  (29 shorter events, 0.3 us)
Async XLA Ops:
  7.2 555.5 %copy-start = (bf16[256,3072]{1,0:T(8,128)(2,1)S(1)}, bf16[256,3072]{1,0:T(8,128)(2,1)}, u32[]{:S(2)}) copy-start(bf16[256,3072]{1,0:T(8,128)(2,1)} %param.22) | copy-start | bytes 4718596
  7.2 173.8 %all-gather.10.cloned.1.call-start = ((), (), s32[]{:S(2)}) async-start(), calls=%async_computation.3 | async-start | bytes 2113536 | tf_op jit(solution)/shard_map/all_gather | solution.py:26
  11.4 174.5 %copy-start.7 = (bf16[8,3072]{1,0:T(8,128)(2,1)S(1)}, bf16[8,3072]{1,0:T(8,128)(2,1)}, u32[]{:S(2)}) copy-start(bf16[8,3072]{1,0:T(8,128)(2,1)} %param.14) | copy-start | bytes 147460
  187.5 3.4 copy-start.1
  187.6 16.7 %copy-start.2 = (f32[3072]{0:T(1024)S(1)}, f32[3072]{0:T(1024)}, u32[]{:S(2)}) copy-start(f32[3072]{0:T(1024)} %param.19) | copy-start | bytes 36868
  207.8 17.0 %copy-start.6 = (s32[8,2]{0,1:T(2,128)S(1)}, s32[8,2]{0,1:T(2,128)}, u32[]{:S(2)}) copy-start(s32[8,2]{0,1:T(2,128)} %param.17) | copy-start | bytes 196
  207.8 323.3 %all-to-all-start = ((bf16[128,8,3072]{2,1,0:T(8,128)(2,1)}), bf16[128,8,3072]{2,1,0:T(8,128)(2,1)}, u32[]{:S(2)}, u32[]{:S(2)}) async-start(bf16[128,8,3072]{2,1,0:T(8,128)(2,1)} %stack.2), calls=%async_computation | async-start | bytes 12582912 | tf_op jit(solution)/shard_map/all_to_all | solution.py:20
  571.5 19.7 %copy-start.4 = (f32[3072]{0:T(1024)S(1)}, f32[3072]{0:T(1024)}, u32[]{:S(2)}) copy-start(f32[3072]{0:T(1024)} %param.23) | copy-start | bytes 36868
  571.5 19.7 %copy-start.5 = (f32[3072]{0:T(1024)S(1)}, f32[3072]{0:T(1024)}, u32[]{:S(2)}) copy-start(f32[3072]{0:T(1024)} %param.24) | copy-start | bytes 36868
  571.5 19.7 %copy-start.3 = (f32[3072,4]{0,1:T(4,128)S(1)}, f32[3072,4]{0,1:T(4,128)}, u32[]{:S(2)}) copy-start(f32[3072,4]{0,1:T(4,128)} %param.20) | copy-start | bytes 147460
  571.5 155.0 %all-to-all-start.2 = ((bf16[128,4,3072]{2,1,0:T(4,128)(2,1)}), bf16[128,4,3072]{2,1,0:T(4,128)(2,1)}, u32[]{:S(2)}, u32[]{:S(2)}) async-start(bf16[128,4,3072]{2,1,0:T(4,128)(2,1)} %reshape.134), calls=%async_computation.2 | async-start | bytes 6291456 | tf_op jit(solution)/shard_map/all_to_all | solution.py:165
Sparse Core Ops, SparseCore 0:
  11.6 169.3 all-gather.9
